TPU v7x, 32 devices: a whole 2x2x4 slice. The times are simulated.
32 devices in a mesh: ctx: 8 (over z, y), tile: 4 (over x, core).
Axes of the slice: x: 2, y: 2, z: 4, core: 2. Of those that a mesh axis runs over, the one named last changes fastest.
Arguments:
- masks: bfloat16 [16, 512, 512], P('ctx', 'tile'), may hold values from 0 to 1
- blur_rows: bfloat16 [512, 512], replicated, may hold values from -0.25 to 0.25
- blur_cols: bfloat16 [512, 512], replicated, may hold values from -0.25 to 0.25
- pupils: float32 [6, 64, 128], replicated, may hold values from -5 to 5
- targets: bfloat16 [16, 512, 512], P('ctx', 'tile'), may hold values from 0 to 1
- context_masters: int32 [16, 12], P('ctx'), may hold values from 0 to 15, as said below
- offsets: int32 [16, 12, 2], P('ctx'), may hold values from 0 to 511
Outputs:
- resist: bfloat16 [16, 512, 512], P('ctx', 'tile')
- mask_grad: float32 [16, 512, 512], P('ctx', 'tile')
Inputs may be any that keep to these rules, and one draw needn't show every extreme that they name: `context_masters`: master m lies on ctx index m // 2. Among the masters named by the 2 contexts of one ctx index there is at most one lying on any one ctx index; a master may be named several times.
All inputs are finite; a program needn't handle non-finite values.
Results may differ from a plain program's by a relative error of at most 0.019.
Values may be sent and summed in bfloat16 or wider, within the bound.
No kernel may reach another device: no remote copies, remote signals or barrier semaphores. Data moves between devices by JAX's collectives and lax.ppermute only.
A program may use at most 64 MiB of HBM per device.

v0:
```python
import math

import jax
import jax.numpy as jnp
from jax import lax
from jax.sharding import PartitionSpec as P

STEEPNESS = 4.0
THRESHOLD = 1.0


def build_tables(extent, mode_count):
    frequency = (jnp.arange(mode_count, dtype=jnp.int32) - mode_count // 2) % extent
    positions = jnp.arange(extent, dtype=jnp.int32)
    windings = frequency[:, None] * positions[None, :] % extent
    angles = windings.astype(jnp.float32) * (2.0 * math.pi / extent)
    scale_factor = 1.0 / math.sqrt(extent)
    cosine_table = jnp.cos(angles) * scale_factor
    sine_table = jnp.sin(angles) * scale_factor
    row_real = cosine_table.astype(jnp.bfloat16)
    row_imag = (-sine_table).astype(jnp.bfloat16)
    col_fwd = jnp.concatenate([cosine_table.T, -sine_table.T], axis=1).astype(jnp.bfloat16)
    inverse_big = jnp.concatenate(
        [
            jnp.concatenate([cosine_table, sine_table], axis=1),
            jnp.concatenate([-sine_table, cosine_table], axis=1),
        ],
        axis=0,
    ).astype(jnp.bfloat16)
    back_real = cosine_table.T.astype(jnp.bfloat16)
    back_imag = sine_table.T.astype(jnp.bfloat16)
    adjoint_big = jnp.concatenate(
        [
            jnp.concatenate([cosine_table.T, -sine_table.T], axis=1),
            jnp.concatenate([sine_table.T, cosine_table.T], axis=1),
        ],
        axis=0,
    ).astype(jnp.bfloat16)
    return (row_real, row_imag, col_fwd, inverse_big, back_real, back_imag, adjoint_big)


def complex_left(left_real, left_imag, values):
    width = values.shape[-1] // 2
    real_lead = jnp.einsum("ux,...xv->...uv", left_real, values, preferred_element_type=jnp.float32)
    imag_lead = jnp.einsum("ux,...xv->...uv", left_imag, values, preferred_element_type=jnp.float32)
    return jnp.concatenate(
        [
            real_lead[..., :width] - imag_lead[..., width:],
            real_lead[..., width:] + imag_lead[..., :width],
        ],
        axis=-1,
    )


def complex_times(factor, values, conjugate):
    width = values.shape[-1] // 2
    factor_real = factor[..., :width]
    factor_imag = factor[..., width:]
    if conjugate:
        factor_imag = -factor_imag
    values_real = values[..., :width]
    values_imag = values[..., width:]
    return jnp.concatenate(
        [
            factor_real * values_real - factor_imag * values_imag,
            factor_real * values_imag + factor_imag * values_real,
        ],
        axis=-1,
    )


def phase_table(shifts, row_begin, band_rows, mode_count, extent):
    freq_u = (jnp.arange(band_rows, dtype=jnp.int32) + row_begin - mode_count // 2) % extent
    freq_v = (jnp.arange(mode_count, dtype=jnp.int32) - mode_count // 2) % extent
    windings = (
        freq_u[None, :, None] * shifts[:, 0][:, None, None]
        + freq_v[None, None, :] * shifts[:, 1][:, None, None]
    ) % extent
    angles = windings.astype(jnp.float32) * (2.0 * math.pi / extent)
    return jnp.concatenate([jnp.cos(angles), -jnp.sin(angles)], axis=-1)


def image_adjoint(
    spectrum, target, pupils, back_real, back_imag, row_real, row_imag, inverse_big, adjoint_big
):
    amplitude = complex_times(pupils, spectrum[None], False).astype(jnp.bfloat16)
    spread = jnp.einsum(
        "kuv,vy->kuy", amplitude, inverse_big, preferred_element_type=jnp.float32
    ).astype(jnp.bfloat16)
    field = complex_left(back_real, back_imag, spread)
    width = field.shape[-1] // 2
    field_real = field[..., :width]
    field_imag = field[..., width:]
    intensity = jnp.sum(field_real * field_real + field_imag * field_imag, axis=0)
    resist = jax.nn.sigmoid(STEEPNESS * (intensity - THRESHOLD))
    slope_term = (resist - target.astype(jnp.float32)) * STEEPNESS * resist * (1.0 - resist)
    pull_back = jnp.concatenate(
        [2.0 * slope_term * field_real, 2.0 * slope_term * field_imag], axis=-1
    ).astype(jnp.bfloat16)
    folded = jnp.einsum(
        "kxy,yv->kxv", pull_back, adjoint_big, preferred_element_type=jnp.float32
    ).astype(jnp.bfloat16)
    grad_amp = complex_left(row_real, row_imag, folded)
    grad_spec = jnp.sum(complex_times(pupils, grad_amp, True), axis=0)
    return (resist.astype(jnp.bfloat16), grad_spec)


def local(masks, blur_rows, blur_cols, pupils, targets, context_masters, offsets):
    ctx_count = lax.axis_size("ctx")
    owned, row_count, extent = masks.shape
    mode_count = pupils.shape[1]
    context_count = context_masters.shape[0]
    source_count = context_masters.shape[1]
    tile_pos = lax.axis_index("tile")
    row_start = tile_pos * row_count
    row_real, row_imag, col_fwd, inverse_big, back_real, back_imag, adjoint_big = build_tables(
        extent, mode_count
    )
    own_row_real = lax.dynamic_slice_in_dim(row_real, row_start, row_count, 1)
    own_row_imag = lax.dynamic_slice_in_dim(row_imag, row_start, row_count, 1)
    own_back_real = lax.dynamic_slice_in_dim(back_real, row_start, row_count, 0)
    own_back_imag = lax.dynamic_slice_in_dim(back_imag, row_start, row_count, 0)
    own_blur = lax.dynamic_slice_in_dim(blur_rows, row_start, row_count, 0)
    own_blur_cols = lax.dynamic_slice_in_dim(blur_rows, row_start, row_count, 1)
    owners = (context_masters // owned).reshape(-1)
    local_index = (context_masters % owned).reshape(-1)
    slot_index = jnp.arange(ctx_count, dtype=jnp.int32)
    owner_match = owners[:, None] == slot_index[None, :]
    wanted = jnp.max(jnp.where(owner_match, local_index[:, None] + 1, 0), axis=0)
    asked_for = lax.all_to_all(wanted[:, None], "ctx", split_axis=0, concat_axis=0, tiled=True)[
        :, 0
    ]
    chosen = asked_for[:, None] == jnp.arange(owned, dtype=jnp.int32)[None, :] + 1
    half_blur = jnp.einsum(
        "mxy,zy->mxz", masks, blur_cols, preferred_element_type=jnp.float32
    ).astype(jnp.bfloat16)
    weights = own_blur
    blurred = jnp.einsum(
        "xj,mjz->mxz",
        weights,
        lax.all_gather(half_blur, "tile", axis=1, tiled=True),
        preferred_element_type=jnp.float32,
    ).astype(jnp.bfloat16)
    column = jnp.einsum("mxy,yv->mxv", blurred, col_fwd, preferred_element_type=jnp.float32).astype(
        jnp.bfloat16
    )
    partial_value = complex_left(own_row_real, own_row_imag, column)
    spectra = lax.psum(partial_value.astype(jnp.bfloat16), "tile")
    outgoing = jnp.einsum(
        "dm,muv->duv", chosen.astype(jnp.bfloat16), spectra, preferred_element_type=jnp.float32
    ).astype(jnp.bfloat16)
    incoming = lax.all_to_all(outgoing, "ctx", split_axis=0, concat_axis=0, tiled=True)
    flat_shift = offsets.reshape(-1, 2)
    picked = jnp.take(incoming, owners, axis=0).astype(jnp.float32)
    turned = complex_times(
        phase_table(flat_shift, 0, mode_count, mode_count, extent), picked, False
    )
    context_spec = jnp.sum(
        turned.reshape(context_count, source_count, mode_count, 2 * mode_count), axis=1
    )

    def one_context(inputs):
        spectrum, target = inputs
        return image_adjoint(
            spectrum,
            target,
            pupils,
            own_back_real,
            own_back_imag,
            own_row_real,
            own_row_imag,
            inverse_big,
            adjoint_big,
        )

    resist, grad_part = lax.map(one_context, (context_spec, targets))
    grad_ctx = lax.psum(grad_part.astype(jnp.bfloat16), "tile").astype(jnp.float32)
    band_start = 0
    repeated = jnp.repeat(grad_ctx, source_count, axis=0)
    back_turn = complex_times(
        phase_table(flat_shift, band_start, mode_count, mode_count, extent), repeated, True
    )
    returned = jnp.einsum(
        "rd,ruv->duv", owner_match.astype(jnp.float32), back_turn, precision=lax.Precision.HIGHEST
    )
    arrived = lax.all_to_all(
        returned.astype(jnp.bfloat16), "ctx", split_axis=0, concat_axis=0, tiled=True
    ).astype(returned.dtype)
    master_grad = jnp.einsum(
        "dm,duv->muv", chosen.astype(jnp.float32), arrived, precision=lax.Precision.HIGHEST
    ).astype(jnp.bfloat16)
    lifted = jnp.einsum(
        "muv,vy->muy", master_grad, inverse_big, preferred_element_type=jnp.float32
    ).astype(jnp.bfloat16)
    surface = (
        jnp.einsum(
            "xu,muy->mxy", own_back_real, lifted[..., :extent], preferred_element_type=jnp.float32
        )
        - jnp.einsum(
            "xu,muy->mxy", own_back_imag, lifted[..., extent:], preferred_element_type=jnp.float32
        )
    ).astype(jnp.bfloat16)
    settled = jnp.einsum(
        "mxy,yz->mxz", surface, blur_cols, preferred_element_type=jnp.float32
    ).astype(jnp.bfloat16)
    weights = own_blur_cols
    mask_grad = jnp.einsum(
        "jx,mjz->mxz",
        weights,
        lax.all_gather(settled, "tile", axis=1, tiled=True),
        preferred_element_type=jnp.float32,
    )
    return (resist, mask_grad)


def solution(mesh):
    placed = (
        P("ctx", "tile", None),
        P(),
        P(),
        P(),
        P("ctx", "tile", None),
        P("ctx", None),
        P("ctx", None, None),
    )
    return jax.shard_map(
        local,
        mesh=mesh,
        in_specs=placed,
        out_specs=(P("ctx", "tile", None), P("ctx", "tile", None)),
        check_vma=False,
    )
```

profile of v0, /device:TPU:0, one launch (start us, length us, event | category | flops | bytes accessed | tf_op | source)
XLA Modules:
  0.0 133.8 jit_solution(16642103256916884030)
XLA Ops:
  7.2 1.0 copy-done
  8.2 2.0 %convolution_convert_fusion.4 = bf16[2,128,512]{2,1,0:T(8,128)(2,1)} fusion(bf16[2,128,512]{2,1,0:T(8,128)(2,1)} %param.9, bf16[512,512]{1,0:T(8,128)(2,1)S(1)} %copy-done), kind=kOutput, calls=%fused_computation.57 | convolution fusion | flops 134348800 | bytes 1048576 | tf_op jit(solution)/shard_map/mxy,zy->mxz/dot_general | solution.py:134
  10.2 0.7 and_select_fusion.1
  11.3 0.7 copy.75
  11.9 7.3 %all-to-all-start = ((s32[8,1,1]{2,1,0:T(1,128)}), s32[8,1,1]{2,1,0:T(1,128)S(1)}, u32[]{:S(2)}, u32[]{:S(2)}) async-start(s32[8,1,1]{2,1,0:T(1,128)} %copy.75), calls=%async_computation | async-start | bytes 8192 | tf_op jit(solution)/shard_map/all_to_all | solution.py:130
  19.3 0.7 copy.73
  20.1 1.1 fusion.45
  22.2 1.1 cosine_multiply_fusion
  23.7 2.0 %all-to-all-done = s32[8,1,1]{2,1,0:T(1,128)S(1)} async-done(((s32[8,1,1]{2,1,0:T(1,128)}), s32[8,1,1]{2,1,0:T(1,128)S(1)}, u32[]{:S(2)}, u32[]{:S(2)}) %all-to-all-start) | async-done | bytes 64 | tf_op jit(solution)/shard_map/all_to_all | solution.py:130
  26.0 3.9 %all-gather.3.cloned.1.call-done = bf16[2,512,512]{2,1,0:T(8,128)(2,1)} async-done(((bf16[2,128,512]{2,1,0:T(8,128)(2,1)}), bf16[2,512,512]{2,1,0:T(8,128)(2,1)}) %all-gather.3.cloned.1.call-update) | async-done | bytes 1048592 | tf_op jit(solution)/shard_map/all_gather | solution.py:141
  29.9 1.9 %fusion.26 = bf16[2,128,128]{2,1,0:T(8,128)(2,1)S(1)} fusion(bf16[2,512,512]{2,1,0:T(8,128)(2,1)} %all-gather.3.cloned.1.call-done, bf16[512,128]{1,0:T(8,128)(2,1)S(1)} %maximum_convert_fusion, bf16[512,512]{1,0:T(8,128)(2,1)S(1)} %copy-done.5, s32[]{:T(128)S(6)} %select_n.140), kind=kOutput, calls=%fused_computation.65 | convolution fusion | flops 167936000 | bytes 1376260 | tf_op jit(solution)/shard_map/mxy,yv->mxv/dot_general | solution.py:144
  32.3 10.4 %psum.14 = bf16[2,64,128]{2,1,0:T(8,128)(2,1)S(1)} all-reduce(bf16[2,64,128]{2,1,0:T(8,128)(2,1)S(1)} %pad_maximum_fusion.1), channel_id=1, replica_groups=mesh['ctx'=8,'tile'=4] {'tile'}, use_global_device_ids=true, to_apply=%region_1.2 | all-reduce | flops 16384 | bytes 65536 | tf_op jit(solution)/shard_map/psum | solution.py:148
  43.0 0.7 copy.79
  43.6 5.7 %all-to-all-start.1 = ((bf16[8,64,128]{2,1,0:T(8,128)(2,1)}), bf16[8,64,128]{2,1,0:T(8,128)(2,1)S(1)}, u32[]{:S(2)}, u32[]{:S(2)}) async-start(bf16[8,64,128]{2,1,0:T(8,128)(2,1)} %copy.79), calls=%async_computation.1 | async-start | bytes 262144 | tf_op jit(solution)/shard_map/all_to_all | solution.py:152
  49.5 7.2 %all-to-all-done.1 = bf16[8,64,128]{2,1,0:T(8,128)(2,1)S(1)} async-done(((bf16[8,64,128]{2,1,0:T(8,128)(2,1)}), bf16[8,64,128]{2,1,0:T(8,128)(2,1)S(1)}, u32[]{:S(2)}, u32[]{:S(2)}) %all-to-all-start.1) | async-done | bytes 131104 | tf_op jit(solution)/shard_map/all_to_all | solution.py:152
  57.6 4.6 %multiply_subtract_fusion.2 = (f32[24,64,64]{2,0,1:T(8,128)S(1)}, f32[24,64,64]{2,0,1:T(8,128)S(1)}) fusion(f32[24,64,128]{2,0,1:T(8,128)S(1)} %fusion.35, s32[24,64]{1,0:T(8,128)S(1)} %get-tuple-element.289, s32[24,64]{0,1:T(8,128)S(1)} %copy.74), kind=kLoop, calls=%fused_computation.79 | loop fusion | flops 2064384 | bytes 1585152 | tf_op jit(solution)/shard_map/sub | solution.py:65
  62.7 0.7 copy-done.4
  63.4 19.3 %while.14 = (s32[]{:T(128)}, bf16[2,128,512]{2,1,0:T(8,128)(2,1)}, bf16[2,64,128]{2,1,0:T(8,128)(2,1)S(1)}, f32[6,64,128]{2,1,0:T(8,128)S(1)}, f32[2,64,128]{2,1...) while((s32[]{:T(128)}, bf16[2,128,512]{2,1,0:T(8,128)(2,1)}, ...), condition=%wide.region_6.7_spmd, body=%wide.region_3.6_spmd.sunk | while | flops 538632192 | bytes 57360672 | solution.py:176
  64.7 0.6 convolution_bitcast_fusion.12
  65.3 1.0 copy-done.1
  66.8 1.2 copy-done.2
  68.5 3.3 %multiply_convert_fusion.4 = (bf16[6,128,512]{1,2,0:T(8,128)(2,1)S(1)}, bf16[6,128,512]{1,2,0:T(8,128)(2,1)S(1)}) fusion(f32[128,512]{0,1:T(8,128)S(1)} %fusion.130, f32[6,128,1024]{1,2,0:T(8,128)} %copy-done.1, f32[6,128,1024]{1,2,0:T(8,128)} %copy-done.2), kind=kLoop, calls=%fused_computation.10.clone.1 | loop fusion | flops 2359296 | bytes 8126464 | tf_op jit(solution)/shard_map/convert
  75.0 1.0 copy-done.1
  76.4 1.2 copy-done.2
  78.2 3.3 %multiply_convert_fusion.4 = (bf16[6,128,512]{1,2,0:T(8,128)(2,1)S(1)}, bf16[6,128,512]{1,2,0:T(8,128)(2,1)S(1)}) fusion(f32[128,512]{0,1:T(8,128)S(1)} %fusion.130, f32[6,128,1024]{1,2,0:T(8,128)} %copy-done.1, f32[6,128,1024]{1,2,0:T(8,128)} %copy-done.2), kind=kLoop, calls=%fused_computation.10.clone.1 | loop fusion | flops 2359296 | bytes 8126464 | tf_op jit(solution)/shard_map/convert
  82.8 10.4 %psum.15 = bf16[2,64,128]{2,1,0:T(8,128)(2,1)S(1)} all-reduce(bf16[2,64,128]{2,1,0:T(8,128)(2,1)S(1)} %get-tuple-element.159), channel_id=1, replica_groups=mesh['ctx'=8,'tile'=4] {'tile'}, use_global_device_ids=true, to_apply=%region_7.8 | all-reduce | flops 16384 | bytes 65536 | tf_op jit(solution)/shard_map/psum | solution.py:177
  93.6 3.7 %multiply_subtract_fusion.1 = (f32[24,64,64]{2,0,1:T(8,128)S(1)}, f32[24,64,64]{2,0,1:T(8,128)S(1)}) fusion(f32[24,64,64]{2,1,0:T(8,128)S(1)} %get-tuple-element.276, f32[24,64,64]{2,1,0:T(8,128)S(1)} %get-tuple-element.275, s32[24,64]{1,0:T(8,128)S(1)} %get-tuple-element.289, s32[24,64]{0,1:T(8,128)S(1)} %copy.74), kind=kLoop, calls=%fused_computation.77 | loop fusion | flops 1966080 | bytes 1585152 | tf_op jit(solution)/shard_map/sub | solution.py:65
  97.8 9.9 %all_to_all.19 = bf16[8,64,128]{2,1,0:T(8,128)(2,1)S(1)} all-to-all(bf16[8,64,128]{2,1,0:T(8,128)(2,1)S(1)} %copy.87), channel_id=1, replica_groups=mesh['ctx'=8,'tile'=4] {'ctx'}, dimensions={0} | all-to-all | bytes 262144 | tf_op jit(solution)/shard_map/all_to_all | solution.py:186
  108.5 1.3 %convolution_convert_fusion.1 = bf16[2,128,512]{2,1,0:T(8,128)(2,1)} fusion(f32[2,512,128]{2,1,0:T(8,128)S(1)} %fusion.52, bf16[512,512]{1,0:T(8,128)(2,1)S(1)} %copy-done, bf16[2,64,1024]{2,1,0:T(8,128)(2,1)S(1)} %convolution_convert_fusion.2, bf16[128,64]{1,0:T(8,128)(2,1)S(1)} %constant_dynamic-slice_fusion.1), kind=kOutput, calls=%fused_computation.54 | convolution fusion | flops 151388160 | bytes 1474560 | tf_op jit(solution)/shard_map/mxy,yz->mxz/dot_general | solution.py:203
  109.8 14.5 %all-gather.5.cloned.1.call-done = bf16[2,512,512]{2,1,0:T(8,128)(2,1)} async-done(((bf16[2,128,512]{2,1,0:T(8,128)(2,1)}), bf16[2,512,512]{2,1,0:T(8,128)(2,1)}) %all-gather.5.cloned.1.call-update) | async-done | bytes 1048592 | tf_op jit(solution)/shard_map/all_gather | solution.py:210
  124.3 1.7 %convolution_bitcast_fusion.4 = f32[2,128,512]{1,2,0:T(8,128)S(1)} fusion(bf16[2,512,512]{2,1,0:T(8,128)(2,1)} %all-gather.5.cloned.1.call-done, bf16[512,512]{1,0:T(8,128)(2,1)S(1)} %copy-done.5, s32[]{:T(128)S(6)} %select_n.140), kind=kOutput, calls=%fused_computation.51 | convolution fusion | flops 134217728 | bytes 1703940 | tf_op jit(solution)/shard_map/jx,mjz->mxz/dot_general | solution.py:207
  126.0 1.0 copy.95
  (98 shorter events, 13.3 us)
Async XLA Ops:
  7.2 1.0 copy-start
  7.2 22.7 %all-gather.3.cloned.1.call-start = ((), (), s32[]{:S(2)}) async-start(), calls=%async_computation.3 | async-start | bytes 1310720 | tf_op jit(solution)/shard_map/all_gather | solution.py:141
  10.2 19.7 %copy-start.5 = (bf16[512,512]{1,0:T(8,128)(2,1)S(1)}, bf16[512,512]{1,0:T(8,128)(2,1)}, u32[]{:S(2)}) copy-start(bf16[512,512]{1,0:T(8,128)(2,1)} %param.10) | copy-start | bytes 1572868
  11.9 13.8 %all-to-all-start = ((s32[8,1,1]{2,1,0:T(1,128)}), s32[8,1,1]{2,1,0:T(1,128)S(1)}, u32[]{:S(2)}, u32[]{:S(2)}) async-start(s32[8,1,1]{2,1,0:T(1,128)} %copy.75), calls=%async_computation | async-start | bytes 8192 | tf_op jit(solution)/shard_map/all_to_all | solution.py:130
  23.6 25.8 %copy-start.3 = (f32[6,64,128]{2,1,0:T(8,128)S(1)}, f32[6,64,128]{2,1,0:T(8,128)}, u32[]{:S(2)}) copy-start(f32[6,64,128]{2,1,0:T(8,128)} %param.12) | copy-start | bytes 589828
  43.6 13.0 %all-to-all-start.1 = ((bf16[8,64,128]{2,1,0:T(8,128)(2,1)}), bf16[8,64,128]{2,1,0:T(8,128)(2,1)S(1)}, u32[]{:S(2)}, u32[]{:S(2)}) async-start(bf16[8,64,128]{2,1,0:T(8,128)(2,1)} %copy.79), calls=%async_computation.1 | async-start | bytes 262144 | tf_op jit(solution)/shard_map/all_to_all | solution.py:152
  49.3 75.0 %all-gather.5.cloned.1.call-start = ((), (), s32[]{:S(2)}) async-start(), calls=%async_computation.4 | async-start | bytes 1310720 | tf_op jit(solution)/shard_map/all_gather | solution.py:210
  62.5 1.0 copy-start.4
  64.7 1.6 %copy-start.1 = (f32[6,128,1024]{1,2,0:T(8,128)}, f32[6,128,1024]{1,2,0:T(8,128)S(1)}, u32[]{:S(2)}) copy-start(f32[6,128,1024]{1,2,0:T(8,128)S(1)} %convolution_bitcast_fusion.11) | copy-start | bytes 9437188 | tf_op jit(solution)/shard_map/while
  66.3 1.7 %copy-start.2 = (f32[6,128,1024]{1,2,0:T(8,128)}, f32[6,128,1024]{1,2,0:T(8,128)S(1)}, u32[]{:S(2)}) copy-start(f32[6,128,1024]{1,2,0:T(8,128)S(1)} %convolution_bitcast_fusion.12) | copy-start | bytes 9437188 | tf_op jit(solution)/shard_map/while
  66.3 1.9 %copy-start.6 = (bf16[2,128,512]{2,1,0:T(8,128)(2,1)S(1)}, bf16[2,128,512]{2,1,0:T(8,128)(2,1)}, u32[]{:S(2)}) copy-start(bf16[2,128,512]{2,1,0:T(8,128)(2,1)} %get-tuple-element.410) | copy-start | bytes 786436 | tf_op jit(solution)/shard_map/while
  68.2 3.6 %copy-start.7 = (bf16[2,128,512]{2,1,0:T(8,128)(2,1)}, bf16[2,128,512]{2,1,0:T(8,128)(2,1)S(1)}, u32[]{:S(2)}) copy-start(bf16[2,128,512]{2,1,0:T(8,128)(2,1)S(1)} %get-tuple-element.426) | copy-start | bytes 786436 | tf_op jit(solution)/shard_map/while
  74.4 1.6 %copy-start.1 = (f32[6,128,1024]{1,2,0:T(8,128)}, f32[6,128,1024]{1,2,0:T(8,128)S(1)}, u32[]{:S(2)}) copy-start(f32[6,128,1024]{1,2,0:T(8,128)S(1)} %convolution_bitcast_fusion.11) | copy-start | bytes 9437188 | tf_op jit(solution)/shard_map/while
  76.0 1.7 %copy-start.2 = (f32[6,128,1024]{1,2,0:T(8,128)}, f32[6,128,1024]{1,2,0:T(8,128)S(1)}, u32[]{:S(2)}) copy-start(f32[6,128,1024]{1,2,0:T(8,128)S(1)} %convolution_bitcast_fusion.12) | copy-start | bytes 9437188 | tf_op jit(solution)/shard_map/while
  76.0 1.9 %copy-start.6 = (bf16[2,128,512]{2,1,0:T(8,128)(2,1)S(1)}, bf16[2,128,512]{2,1,0:T(8,128)(2,1)}, u32[]{:S(2)}) copy-start(bf16[2,128,512]{2,1,0:T(8,128)(2,1)} %get-tuple-element.410) | copy-start | bytes 786436 | tf_op jit(solution)/shard_map/while
  77.9 3.6 %copy-start.7 = (bf16[2,128,512]{2,1,0:T(8,128)(2,1)}, bf16[2,128,512]{2,1,0:T(8,128)(2,1)S(1)}, u32[]{:S(2)}) copy-start(bf16[2,128,512]{2,1,0:T(8,128)(2,1)S(1)} %get-tuple-element.426) | copy-start | bytes 786436 | tf_op jit(solution)/shard_map/while
Sparse Core Ops, SparseCore 0:
  10.3 19.4 all-gather.2
  110.0 14.2 all-gather.4
where the time goes:
time: 134 us
  blocking collectives  30.8 us (23%)
  waiting for transfers between devices  27.6 us (21%)
  other arithmetic  22.2 us (17%)
  between operations  14.3 us (11%)
  matrix products  13.9 us (10%)
  starting transfers between devices  13.1 us (10%)
  local copies, waits for them, and re-layouts  11.7 us (9%)
    all_gather x1, waiting for transfers between devices, local(): lax.all_gather(settled, 'tile', axis=1, tiled=True)  14.5 us
    psum x1, blocking collectives, local(): lax.psum(grad_part.astype(jnp.bfloat16), 'tile').astype(jnp.float32)  10.4 us
    psum x1, blocking collectives, local(): spectra = lax.psum(partial_value.astype(jnp.bfloat16), 'tile')  10.4 us
    all_to_all x1, blocking collectives, local(): lax.all_to_all(returned.astype(jnp.bfloat16), 'ctx', split_axis=0, concat...  9.92 us
    sub x4, other arithmetic, complex_times(): factor_real * values_real - factor_imag * values_imag  8.65 us
    another operation x6, other arithmetic  7.55 us
    all_to_all x1, starting transfers between devices, local(): lax.all_to_all(wanted[:, None], 'ctx', split_axis=0, concat_axis=0, tiled...  7.31 us
    all_to_all x1, waiting for transfers between devices, local(): lax.all_to_all(outgoing, 'ctx', split_axis=0, concat_axis=0, tiled=True)  7.17 us
  transfers between devices with their start and end apart: 4, of which 4 were waited for; matrix products, arithmetic and copies ran while one was open for 5% of the time, Pallas kernels for 0%

commit v1 on v0

v1 whole, which is shorter than its diff:
```python
import functools
import math

import jax
import jax.numpy as jnp
import numpy as np
from jax import lax
from jax.experimental import pallas as pl
from jax.experimental.pallas import tpu as pltpu
from jax.sharding import Mesh
from jax.sharding import PartitionSpec as P

STEEPNESS = 4.0
THRESHOLD = 1.0
BF16 = jnp.bfloat16
F32 = jnp.float32
VMEM_BYTES = 40 << 20


def params(limit=VMEM_BYTES):
    return pltpu.CompilerParams(vmem_limit_bytes=limit)


def vmem_specs(count):
    return [pl.BlockSpec(memory_space=pltpu.VMEM)] * count


def dft_tables(extent, modes):
    frequency = np.arange(modes) - modes // 2
    windings = (frequency[:, None] * np.arange(extent)[None, :]) % extent
    angles = windings.astype(np.float32) * np.float32(2.0 * math.pi / extent)
    scale = 1.0 / math.sqrt(extent)
    cosine = (np.cos(angles) * np.float32(scale)).astype(BF16)
    sine = (np.sin(angles) * np.float32(scale)).astype(BF16)
    forward = np.concatenate([cosine, -sine], axis=0)
    points = np.concatenate([cosine.T, sine.T], axis=1)
    inverse = np.concatenate(
        [np.concatenate([cosine, sine], axis=1), np.concatenate([-sine, cosine], axis=1)], axis=0
    )
    return forward, points, inverse, np.ascontiguousarray(inverse.T)


def dot(a, b):
    return lax.dot_general(a, b, (((1,), (0,)), ((), ())), preferred_element_type=F32)


def dot_nt(a, b):
    return lax.dot_general(a, b, (((1,), (1,)), ((), ())), preferred_element_type=F32)


def dot_tn(a, b):
    return lax.dot_general(a, b, (((0,), (0,)), ((), ())), preferred_element_type=F32)


def left_half(shape):
    return lax.broadcasted_iota(jnp.int32, shape, len(shape) - 1) < shape[-1] // 2


def swap(x):
    return pltpu.roll(x, x.shape[-1] // 2, x.ndim - 1)


def times_i(x):
    turned = swap(x)
    return jnp.where(left_half(x.shape), -turned, turned)


def tile_index(axes):
    return lax.axis_index(axes[0]) * lax.axis_size(axes[1]) + lax.axis_index(axes[1])


def spectrum_kernel(where_ref, masks_ref, br_ref, bc_ref, fwd_ref, keep_ref, send_ref, a_ref, c_ref, full_ref):
    owned, rows, extent = masks_ref.shape
    modes = fwd_ref.shape[0] // 2
    band = modes // 2
    tile_pos = where_ref[0]
    side = where_ref[1]
    own_cols = br_ref[:, pl.ds(pl.multiple_of(tile_pos * rows, rows), rows)]
    c = dot(fwd_ref[...], bc_ref[...]).astype(BF16)
    a = dot(fwd_ref[...], own_cols).astype(BF16)
    c_ref[...] = c
    a_ref[...] = a
    folded = dot_nt(masks_ref[...].reshape(owned * rows, extent), c)
    turned = times_i(folded).astype(BF16)
    folded = folded.astype(BF16)
    for m in range(owned):
        part = slice(m * rows, (m + 1) * rows)
        full_ref[m] = dot(a[:modes], folded[part]) + dot(a[modes:], turned[part])
    keep_ref[...] = full_ref[:, pl.ds(pl.multiple_of(side * band, band), band), :]
    send_ref[...] = full_ref[:, pl.ds(pl.multiple_of((1 - side) * band, band), band), :]


def phase_kernel(where_ref, masters_ref, offsets_ref, w1_ref, w2_ref, *, sources, extent):
    contexts, masters, band, width = w1_ref.shape
    modes = width // 2
    side = where_ref[1]
    w1_ref[...] = jnp.zeros_like(w1_ref)
    w2_ref[...] = jnp.zeros_like(w2_ref)
    count = contexts * sources
    step = 2.0 * math.pi / extent
    freq_u = lax.broadcasted_iota(jnp.int32, (band, 128), 0) + side * band - modes // 2
    lane = lax.broadcasted_iota(jnp.int32, (1, 128), 1)
    row = lax.broadcasted_iota(jnp.int32, (count, 1), 0)
    shift_r = jnp.zeros((1, 128), jnp.int32)
    shift_s = jnp.zeros((count, 1), jnp.int32)
    for j in range(count):
        shift_r = jnp.where(lane == j, offsets_ref[2 * j], shift_r)
        shift_s = jnp.where(row == j, offsets_ref[2 * j + 1], shift_s)
    angle_u = ((freq_u * shift_r) & (extent - 1)).astype(F32) * step
    lanes = lax.broadcasted_iota(jnp.int32, (count, width), 1)
    freq_v = (lanes & (modes - 1)) - modes // 2
    angle_v = ((freq_v * shift_s) & (extent - 1)).astype(F32) * step
    p_re, p_im = jnp.cos(angle_u), -jnp.sin(angle_u)
    q_re, q_im = jnp.cos(angle_v), -jnp.sin(angle_v)
    left = left_half((count, width))
    signed_im = jnp.where(left, q_im, -q_im)
    signed_re = jnp.where(left, q_re, -q_re)
    for c in range(contexts):
        for j in range(sources):
            i = c * sources + j
            m = masters_ref[i]
            re = jnp.broadcast_to(p_re[:, i : i + 1], (band, width))
            im = jnp.broadcast_to(p_im[:, i : i + 1], (band, width))
            one = slice(i, i + 1)
            w1_ref[c, m] = w1_ref[c, m] + re * q_re[one] - im * q_im[one]
            w2_ref[c, m] = w2_ref[c, m] + re * signed_im[one] + im * signed_re[one]


def over_masters(count, body, init):
    if count <= 16:
        for i in range(count):
            init = body(i, init)
        return init
    return lax.fori_loop(0, count, body, init)


def context_kernel(got_ref, w1_ref, w2_ref, spec_ref):
    owners, halves, owned, band, width = got_ref.shape
    contexts = w1_ref.shape[0]

    def body(d, sums):
        sums = list(sums)
        for m in range(owned):
            value = got_ref[d, 0, m].astype(F32)
            for h in range(1, halves):
                value = value + got_ref[d, h, m].astype(F32)
            for c in range(contexts):
                sums[2 * c] = sums[2 * c] + value * w1_ref[c, d * owned + m]
                sums[2 * c + 1] = sums[2 * c + 1] + value * w2_ref[c, d * owned + m]
        return tuple(sums)

    zero = jnp.zeros((band, width), F32)
    sums = over_masters(owners, body, (zero,) * (2 * contexts))
    for c in range(contexts):
        spec_ref[c] = sums[2 * c] + swap(sums[2 * c + 1])


def join_bands(full_ref, side, mine, other):
    band = mine.shape[-2]
    full_ref[:, pl.ds(pl.multiple_of(side * band, band), band), :] = mine
    full_ref[:, pl.ds(pl.multiple_of((1 - side) * band, band), band), :] = other


def image_kernel(
    where_ref, mine_ref, other_ref, pupils_ref, targets_ref, fwd_ref, points_ref, inv_ref, adj_ref,
    resist_ref, keep_ref, send_ref,
    spec_ref, left_ref, field_ref, pull_ref,
):
    kernels, modes, width = pupils_ref.shape
    contexts, rows, extent = targets_ref.shape
    band = modes // 2
    tile_pos = where_ref[0]
    side = where_ref[1]
    join_bands(spec_ref, side, mine_ref[...], other_ref[...])
    own = pl.ds(pl.multiple_of(tile_pos * rows, rows), rows)
    points = points_ref[own, :]
    own_fwd = jnp.concatenate([fwd_ref[:modes, own], fwd_ref[modes:, own]], axis=1)
    left = left_half((modes, width))

    def pupil_parts(k):
        pupil = pupils_ref[k]
        turned = swap(pupil)
        return jnp.where(left, pupil, turned), jnp.where(left, -turned, pupil)

    block = 16

    def one_context(c, carry):
        spec = spec_ref[c]
        spec_turned = swap(spec)
        for k in range(kernels):
            same, cross = pupil_parts(k)
            amp = spec * same + spec_turned * cross
            stack = jnp.concatenate([amp.astype(BF16), times_i(amp).astype(BF16)], axis=0)
            left_ref[k * rows : (k + 1) * rows, :] = dot(points, stack).astype(BF16)
        field_ref[...] = dot(left_ref[...], inv_ref[...])

        def one_block(b, carry):
            begin = pl.multiple_of(b * block, block)
            intensity = jnp.zeros((block, extent), F32)
            for k in range(kernels):
                re = field_ref[pl.ds(k * rows + begin, block), :extent]
                im = field_ref[pl.ds(k * rows + begin, block), extent:]
                intensity = intensity + re * re + im * im
            resist = jax.nn.sigmoid(STEEPNESS * (intensity - THRESHOLD))
            target = targets_ref[c, pl.ds(begin, block), :].astype(F32)
            slope = (resist - target) * (2.0 * STEEPNESS) * resist * (1.0 - resist)
            resist_ref[c, pl.ds(begin, block), :] = resist.astype(BF16)
            for k in range(kernels):
                at = pl.ds(k * rows + begin, block)
                pull_ref[at, :extent] = (slope * field_ref[at, :extent]).astype(BF16)
                pull_ref[at, extent:] = (slope * field_ref[at, extent:]).astype(BF16)
            return carry

        lax.fori_loop(0, rows // block, one_block, 0)
        folded = dot(pull_ref[...], adj_ref[...])
        total = jnp.zeros((modes, width), F32)
        for k in range(kernels):
            same, cross = pupil_parts(k)
            part = folded[k * rows : (k + 1) * rows]
            stack = jnp.concatenate([part.astype(BF16), times_i(part).astype(BF16)], axis=0)
            grad = dot(own_fwd, stack)
            total = total + grad * same - swap(grad) * cross
        spec_ref[c] = total
        return carry

    lax.fori_loop(0, contexts, one_context, 0)
    keep_ref[...] = spec_ref[:, pl.ds(pl.multiple_of(side * band, band), band), :]
    send_ref[...] = spec_ref[:, pl.ds(pl.multiple_of((1 - side) * band, band), band), :]


def scatter_kernel(mine_ref, other_ref, w1_ref, w2_ref, out_ref):
    owners, halves, owned, band, width = out_ref.shape
    contexts = w1_ref.shape[0]
    grads = [mine_ref[c] + other_ref[c] for c in range(contexts)]
    turned = [swap(grad) for grad in grads]

    def body(d, carry):
        for m in range(owned):
            value = jnp.zeros((band, width), F32)
            for c in range(contexts):
                value = value + grads[c] * w1_ref[c, d * owned + m] + turned[c] * w2_ref[c, d * owned + m]
            value = value.astype(BF16)
            for h in range(halves):
                out_ref[d, h, m] = value
        return carry

    over_masters(owners, body, 0)


def gather_kernel(got_ref, out_ref):
    owners, halves, owned, band, width = got_ref.shape

    def body(d, sums):
        return tuple(
            sum((got_ref[d, h, m].astype(F32) for h in range(halves)), sums[m]) for m in range(owned)
        )

    sums = over_masters(owners, body, (jnp.zeros((band, width), F32),) * owned)
    for m in range(owned):
        out_ref[m] = sums[m].astype(out_ref.dtype)


def lift_kernel(where_ref, mine_ref, other_ref, a_ref, c_ref, out_ref, full_ref):
    owned = out_ref.shape[0]
    side = where_ref[1]
    join_bands(full_ref, side, mine_ref[...], other_ref[...])
    for m in range(owned):
        grad = full_ref[m]
        stack = jnp.concatenate([grad.astype(BF16), (-times_i(grad)).astype(BF16)], axis=0)
        lifted = dot_tn(a_ref[...], stack).astype(BF16)
        out_ref[m] = dot(lifted, c_ref[...])


def local(masks, blur_rows, blur_cols, pupils, targets, context_masters, offsets):
    owned, rows, extent = masks.shape
    kernels, modes, width = pupils.shape
    contexts, sources = context_masters.shape
    owners = lax.axis_size("ctx")
    halves = lax.axis_size("hi")
    band = modes // 2
    masters = owners * owned
    tables = dft_tables(extent, modes)
    forward, points, inverse, adjoint = (jnp.asarray(table) for table in tables)
    where = jnp.stack([tile_index(("hi", "lo")), lax.axis_index("lo")]).astype(jnp.int32)
    smem = pl.BlockSpec(memory_space=pltpu.SMEM)
    vmem = pl.BlockSpec(memory_space=pltpu.VMEM)
    band_f32 = jax.ShapeDtypeStruct((owned, band, width), F32)
    ctx_f32 = jax.ShapeDtypeStruct((contexts, band, width), F32)

    def swap_sides(x):
        return lax.ppermute(x, "lo", [(0, 1), (1, 0)])

    def exchange(x):
        flat = x.reshape((owners * halves,) + x.shape[2:])
        got = lax.all_to_all(flat, ("ctx", "hi"), split_axis=0, concat_axis=0, tiled=True)
        return got.reshape(x.shape)

    keep, send, a_table, c_table = pl.pallas_call(
        spectrum_kernel,
        out_shape=(
            band_f32,
            band_f32,
            jax.ShapeDtypeStruct((width, rows), BF16),
            jax.ShapeDtypeStruct((width, extent), BF16),
        ),
        in_specs=[smem] + [vmem] * 4,
        out_specs=(vmem,) * 4,
        scratch_shapes=[pltpu.VMEM((owned, modes, width), F32)],
        compiler_params=params(),
        cost_estimate=pl.CostEstimate(flops=400_000_000, bytes_accessed=2_000_000, transcendentals=0),
    )(where, masks, blur_rows, blur_cols, forward)
    spectra = (keep + swap_sides(send)).astype(BF16)
    outgoing = jnp.broadcast_to(spectra[None, None], (owners, halves, owned, band, width))
    incoming = exchange(outgoing)

    w_shape = jax.ShapeDtypeStruct((contexts, masters, band, width), F32)
    w1, w2 = pl.pallas_call(
        functools.partial(phase_kernel, sources=sources, extent=extent),
        out_shape=(w_shape, w_shape),
        in_specs=[smem] * 3,
        out_specs=(vmem,) * 2,
        compiler_params=params(),
        cost_estimate=pl.CostEstimate(flops=100_000_000, bytes_accessed=1_000_000, transcendentals=0),
    )(where, context_masters.reshape(-1), offsets.reshape(-1))

    spec = pl.pallas_call(
        context_kernel,
        out_shape=ctx_f32,
        in_specs=[vmem] * 3,
        out_specs=vmem,
        compiler_params=params(),
        cost_estimate=pl.CostEstimate(flops=10_000_000, bytes_accessed=1_000_000, transcendentals=0),
    )(incoming, w1, w2)

    resist, keep, send = pl.pallas_call(
        image_kernel,
        out_shape=(jax.ShapeDtypeStruct((contexts, rows, extent), BF16), ctx_f32, ctx_f32),
        in_specs=[smem] + [vmem] * 8,
        out_specs=(vmem,) * 3,
        scratch_shapes=[
            pltpu.VMEM((contexts, modes, width), F32),
            pltpu.VMEM((kernels * rows, width), BF16),
            pltpu.VMEM((kernels * rows, 2 * extent), F32),
            pltpu.VMEM((kernels * rows, 2 * extent), BF16),
        ],
        compiler_params=params(),
        cost_estimate=pl.CostEstimate(flops=2_000_000_000, bytes_accessed=2_000_000, transcendentals=0),
    )(where, spec, swap_sides(spec), pupils, targets, forward, points, inverse, adjoint)

    returned = pl.pallas_call(
        scatter_kernel,
        out_shape=jax.ShapeDtypeStruct((owners, halves, owned, band, width), BF16),
        in_specs=[vmem] * 4,
        out_specs=vmem,
        compiler_params=params(),
        cost_estimate=pl.CostEstimate(flops=10_000_000, bytes_accessed=1_000_000, transcendentals=0),
    )(keep, swap_sides(send), w1, w2)
    arrived = exchange(returned)
    master_grad = pl.pallas_call(
        gather_kernel,
        out_shape=band_f32,
        in_specs=[vmem],
        out_specs=vmem,
        compiler_params=params(),
        cost_estimate=pl.CostEstimate(flops=10_000_000, bytes_accessed=1_000_000, transcendentals=0),
    )(arrived)
    mask_grad = pl.pallas_call(
        lift_kernel,
        out_shape=jax.ShapeDtypeStruct((owned, rows, extent), F32),
        in_specs=[smem] + [vmem] * 4,
        out_specs=vmem,
        scratch_shapes=[pltpu.VMEM((owned, modes, width), F32)],
        compiler_params=params(),
        cost_estimate=pl.CostEstimate(flops=100_000_000, bytes_accessed=1_000_000, transcendentals=0),
    )(where, master_grad, swap_sides(master_grad), a_table, c_table)
    return resist, mask_grad


def solution(mesh):
    devices = mesh.devices
    contexts, tiles = devices.shape
    fine = Mesh(devices.reshape(contexts, tiles // 2, 2), ("ctx", "hi", "lo"))
    rows = ("hi", "lo")
    placed = (
        P("ctx", rows, None),
        P(),
        P(),
        P(),
        P("ctx", rows, None),
        P("ctx", None),
        P("ctx", None, None),
    )
    return jax.shard_map(
        local,
        mesh=fine,
        in_specs=placed,
        out_specs=(P("ctx", rows, None), P("ctx", rows, None)),
        check_vma=False,
    )
```

time: 134 us -> 53.4 us (0.40)
  other arithmetic: 22.2 us -> 0.08 us
  blocking collectives: 30.8 us -> 13.5 us
  waiting for transfers between devices: 27.6 us -> 13.2 us
  matrix products: 13.9 us -> 0 us
  between operations: 14.3 us -> 0.75 us
  Pallas kernels: 0 us -> 11.1 us
  local copies, waits for them, and re-layouts: 11.7 us -> 5 us
  starting transfers between devices: 13.1 us -> 9.25 us
    psum x2 -> x0, blocking collectives: 20.8 us -> none  [the longest x1 10.4 us: local(): lax.psum(grad_part.astype(jnp.bfloat16), 'tile').astype(jnp.float32)]
    all_gather x2 -> x0, waiting for transfers between devices: 18.3 us -> none  [the longest x1 14.5 us: local(): lax.all_gather(settled, 'tile', axis=1, tiled=True)]
    dot_general x23 -> x0, matrix products: 13.9 us -> none  [the longest x1 1.99 us: local(): jnp.einsum('mxy,zy->mxz', masks, blur_cols, preferred_element_type=jnp.fl...]
    pallas_call x0 -> x7, Pallas kernels: none -> 11.1 us  [the longest x1 6.71 us: local(): pl.pallas_call(image_kernel, out_shape=(jax.ShapeDtypeStruct((contexts, r...]
    sub x4 -> x0, other arithmetic: 8.65 us -> none  [complex_times(): factor_real * values_real - factor_imag * values_imag]
    another operation x6 -> x1, other arithmetic: 7.55 us -> 0.08 us  [local(): jnp.stack([tile_index(('hi', 'lo')), lax.axis_index('lo')])]
    all_to_all x2 -> x1, starting transfers between devices: 13 us -> 8.33 us  [exchange(): lax.all_to_all(flat, ('ctx', 'hi'), split_axis=0, concat_axis=0, tiled=True)]
    while x18 -> x0, local copies, waits for them, and re-layouts: 4.61 us -> none
  transfers between devices with their start and end apart: 4 -> 5, of which waited for: 4 -> 5; matrix products, arithmetic and copies ran while one was open for 5% -> 1% of each run, Pallas kernels for 0% -> 2%
where the time goes in v1:
time: 53.4 us; the launch traced here: 53 us
  blocking collectives  13.5 us (25%)
  waiting for transfers between devices  13.2 us (25%)
  Pallas kernels  11.1 us (21%)
  starting transfers between devices  9.25 us (17%)
  local copies, waits for them, and re-layouts  5 us (9%)
  between operations  0.75 us (1%)
    all_to_all x1, blocking collectives, exchange(): lax.all_to_all(flat, ('ctx', 'hi'), split_axis=0, concat_axis=0, tiled=True)  13.5 us
    all_to_all x1, waiting for transfers between devices, exchange(): lax.all_to_all(flat, ('ctx', 'hi'), split_axis=0, concat_axis=0, tiled=True)  8.93 us
    all_to_all x1, starting transfers between devices, exchange(): lax.all_to_all(flat, ('ctx', 'hi'), split_axis=0, concat_axis=0, tiled=True)  8.33 us
    pallas_call x1, Pallas kernels, local(): pl.pallas_call(image_kernel, out_shape=(jax.ShapeDtypeStruct((contexts, r...  6.71 us
    ppermute x4, waiting for transfers between devices, swap_sides(): return lax.ppermute(x, 'lo', [(0, 1), (1, 0)])  4.3 us
    unnamed x25, local copies, waits for them, and re-layouts  4.07 us
    pallas_call x1, Pallas kernels, local(): pl.pallas_call(lift_kernel, out_shape=jax.ShapeDtypeStruct((owned, rows,...  1.86 us
    pallas_call x1, Pallas kernels, local(): pl.pallas_call(spectrum_kernel, out_shape=(band_f32, band_f32, jax.ShapeD...  1.25 us
  transfers between devices with their start and end apart: 5, of which 5 were waited for; matrix products, arithmetic and copies ran while one was open for 1% of the time, Pallas kernels for 2%

profile of v1, /device:TPU:0, one launch (start us, length us, event | category | flops | bytes accessed | tf_op | source)
XLA Modules:
  0.0 53.0 jit_solution(15760329970644883432)
XLA Ops:
  0.6 0.1 pad_add_fusion.where_ref
  0.7 1.0 %copy-done = bf16[512,512]{1,0:T(8,128)(2,1)S(1)} copy-done((bf16[512,512]{1,0:T(8,128)(2,1)S(1)}, bf16[512,512]{1,0:T(8,128)(2,1)}, u32[]{:S(2)}) %copy-start) | copy-done | bytes 524312
  1.8 1.0 %copy-done.1 = bf16[512,512]{1,0:T(8,128)(2,1)S(1)} copy-done((bf16[512,512]{1,0:T(8,128)(2,1)S(1)}, bf16[512,512]{1,0:T(8,128)(2,1)}, u32[]{:S(2)}) %copy-start.1) | copy-done | bytes 524312
  2.8 0.9 %copy-done.2 = bf16[2,128,512]{2,1,0:T(8,128)(2,1)S(1)} copy-done((bf16[2,128,512]{2,1,0:T(8,128)(2,1)S(1)}, bf16[2,128,512]{2,1,0:T(8,128)(2,1)}, u32[]{:S(2)}) %copy-start.2) | copy-done | bytes 262168
  3.7 0.9 %copy-done.7 = bf16[128,512]{1,0:T(8,128)(2,1)S(1)} copy-done((bf16[128,512]{1,0:T(8,128)(2,1)S(1)}, bf16[128,512]{1,0:T(8,128)(2,1)}, u32[]{:S(2)}) %copy-start.7) | copy-done | bytes 131096
  4.7 1.2 %shard_map.122 = (f32[2,32,128]{2,1,0:T(8,128)S(1)}, f32[2,32,128]{2,1,0:T(8,128)S(1)}, bf16[128,128]{1,0:T(8,128)(2,1)S(1)}, bf16[128,512]{1,0:T(8,128)(2,1)S(1)}) custom-call(s32[2]{0:T(128)S(1)} %pad_add_fusion.where_ref, bf16[2,128,512]{2,1,0:T(8,128)(2,1)S(1)} %copy-done.2, bf16[512,512]{1,0:T(8,128)(2,1)S(1)} %copy-done, ...), custom_call_target="tpu_custom_call" | custom-call | flops 400000000 | bytes 2000000 | tf_op jit(solution)/shard_map/pallas_call | solution.py:298
  5.9 0.6 %collective-permute-start = (f32[2,32,128]{2,1,0:T(8,128)S(1)}, f32[2,32,128]{2,1,0:T(8,128)S(1)}, u32[]{:S(2)}, u32[]{:S(2)}) collective-permute-start(f32[2,32,128]{2,1,0:T(8,128)S(1)} %get-tuple-element.12), channel_id=1, source_target_pairs={{0,1},{1,0},{2,3},{3,2},{4,5},{5,4},{6,7},{7,6},{8,9},{9,8},{10,11... | collective-permute-start | bytes 98312 | tf_op jit(solution)/shard_map/ppermute | solution.py:291
  6.5 0.9 %collective-permute-done = f32[2,32,128]{2,1,0:T(8,128)S(1)} collective-permute-done((f32[2,32,128]{2,1,0:T(8,128)S(1)}, f32[2,32,128]{2,1,0:T(8,128)S(1)}, u32[]{:S(2)}, u32[]{:S(2)}) %collective-permute-start) | collective-permute-done | bytes 32800 | tf_op jit(solution)/shard_map/ppermute | solution.py:291
  7.3 0.8 %reshape.23 = bf16[16,2,32,128]{3,2,1,0:T(8,128)(2,1)} broadcast(bf16[2,32,128]{2,1,0:T(8,128)(2,1)S(1)} %add_convert_fusion), dimensions={1,2,3} | broadcast | bytes 278528 | tf_op jit(solution)/shard_map/reshape | solution.py:294
  8.1 8.3 %all-to-all-start = ((bf16[16,2,32,128]{3,2,1,0:T(8,128)(2,1)}), bf16[16,2,32,128]{3,2,1,0:T(8,128)(2,1)S(1)}, u32[]{:S(2)}, u32[]{:S(2)}) async-start(bf16[16,2,32,128]{3,2,1,0:T(8,128)(2,1)} %reshape.23), calls=%async_computation | async-start | bytes 524288 | tf_op jit(solution)/shard_map/all_to_all | solution.py:295
  16.4 0.0 copy-done.11
  16.4 0.1 reshape.25.masters_ref
  16.5 0.0 copy-done.10
  16.5 0.1 copy.14
  16.6 0.1 reshape.26.offsets_ref
  16.7 1.0 %shard_map.123 = (f32[2,16,32,128]{3,2,1,0:T(8,128)S(1)}, f32[2,16,32,128]{3,2,1,0:T(8,128)S(1)}) custom-call(s32[2]{0:T(128)S(1)} %pad_add_fusion.where_ref, s32[24]{0:T(128)S(1)} %reshape.25.masters_ref, s32[48]{0:T(128)S(1)} %reshape.26.offsets_ref), custom_call_target="tpu_custom_call" | custom-call | flops 100000000 | bytes 1000000 | tf_op jit(solution)/shard_map/pallas_call | solution.py:317
  17.7 8.9 %all-to-all-done = bf16[16,2,32,128]{3,2,1,0:T(8,128)(2,1)S(1)} async-done(((bf16[16,2,32,128]{3,2,1,0:T(8,128)(2,1)}), bf16[16,2,32,128]{3,2,1,0:T(8,128)(2,1)S(1)}, u32[]{:S(2)}, u32[]{:S(2)}) %all-to-all-start) | async-done | bytes 262176 | tf_op jit(solution)/shard_map/all_to_all | solution.py:295
  26.6 0.0 copy-start.8
  26.7 0.0 copy-start.9
  26.7 0.1 shard_map.124.mine_ref
  26.8 0.1 collective-permute-start.1
  26.9 1.2 %collective-permute-done.1.other_ref = f32[2,32,128]{2,1,0:T(8,128)S(1)} collective-permute-done((f32[2,32,128]{2,1,0:T(8,128)S(1)}, f32[2,32,128]{2,1,0:T(8,128)S(1)}, u32[]{:S(2)}, u32[]{:S(2)}) %collective-permute-start.1) | collective-permute-done | bytes 32800 | tf_op jit(solution)/shard_map/ppermute | solution.py:291
  28.1 0.0 copy-done.3
  28.1 0.0 copy-done.4
  28.1 6.7 %shard_map.125 = (bf16[2,128,512]{2,1,0:T(8,128)(2,1)}, f32[2,32,128]{2,1,0:T(8,128)S(1)}, f32[2,32,128]{2,1,0:T(8,128)S(1)}) custom-call(s32[2]{0:T(128)S(1)} %pad_add_fusion.where_ref, f32[2,32,128]{2,1,0:T(8,128)S(1)} %shard_map.124.mine_ref, f32[2,32,128]{2,1,0:T(8,128)S(1)} %collective-permute-done.1.other_ref, f32[6,64,128]{2,1,0:T(8,128)S(1)} %copy-done.4, ...), custom_call_target="tpu_custom_call" | custom-call | flops 2000000000 | bytes 2000000 | tf_op jit(solution)/shard_map/pallas_call | solution.py:335
  34.8 0.2 collective-permute-start.2
  35.0 1.1 %collective-permute-done.2.other_ref = f32[2,32,128]{2,1,0:T(8,128)S(1)} collective-permute-done((f32[2,32,128]{2,1,0:T(8,128)S(1)}, f32[2,32,128]{2,1,0:T(8,128)S(1)}, u32[]{:S(2)}, u32[]{:S(2)}) %collective-permute-start.2) | collective-permute-done | bytes 32800 | tf_op jit(solution)/shard_map/ppermute | solution.py:291
  36.1 0.1 shard_map.126
  36.2 13.5 %all_to_all.10 = bf16[16,2,32,128]{3,2,1,0:T(8,128)(2,1)S(1)} all-to-all(bf16[16,2,32,128]{3,2,1,0:T(8,128)(2,1)S(1)} %bitcast.7), channel_id=1, replica_groups=mesh['ctx'=8,'hi'=2,'lo'=2] {'ctx','hi'}, dimensions={0} | all-to-all | bytes 524288 | tf_op jit(solution)/shard_map/all_to_all | solution.py:295
  49.8 0.1 collective-permute-start.3
  49.9 1.2 %collective-permute-done.3.other_ref = f32[2,32,128]{2,1,0:T(8,128)S(1)} collective-permute-done((f32[2,32,128]{2,1,0:T(8,128)S(1)}, f32[2,32,128]{2,1,0:T(8,128)S(1)}, u32[]{:S(2)}, u32[]{:S(2)}) %collective-permute-start.3) | collective-permute-done | bytes 32800 | tf_op jit(solution)/shard_map/ppermute | solution.py:291
  51.1 1.9 %shard_map.128 = f32[2,128,512]{2,1,0:T(8,128)} custom-call(s32[2]{0:T(128)S(1)} %pad_add_fusion.where_ref, f32[2,32,128]{2,1,0:T(8,128)S(1)} %shard_map.127.mine_ref, f32[2,32,128]{2,1,0:T(8,128)S(1)} %collective-permute-done.3.other_ref, bf16[128,128]{1,0:T(8,128)(2,1)S(1)} %get-tuple-element.18.a_ref, bf16[128,512]{1,0:T(8,128)(2,1)S(1)} %get-tuple-element.19.c_ref), custom_call_target="tpu_custom_call" | custom-call | flops 100000000 | bytes 1000000 | tf_op jit(solution)/shard_map/pallas_call | solution.py:367
  (16 shorter events, 0.1 us)
Async XLA Ops:
  0.7 1.0 %copy-start = (bf16[512,512]{1,0:T(8,128)(2,1)S(1)}, bf16[512,512]{1,0:T(8,128)(2,1)}, u32[]{:S(2)}) copy-start(bf16[512,512]{1,0:T(8,128)(2,1)} %br_ref.1) | copy-start | bytes 1572868
  1.8 1.0 %copy-start.1 = (bf16[512,512]{1,0:T(8,128)(2,1)S(1)}, bf16[512,512]{1,0:T(8,128)(2,1)}, u32[]{:S(2)}) copy-start(bf16[512,512]{1,0:T(8,128)(2,1)} %bc_ref.1) | copy-start | bytes 1572868
  2.8 0.9 %copy-start.2 = (bf16[2,128,512]{2,1,0:T(8,128)(2,1)S(1)}, bf16[2,128,512]{2,1,0:T(8,128)(2,1)}, u32[]{:S(2)}) copy-start(bf16[2,128,512]{2,1,0:T(8,128)(2,1)} %masks_ref.1) | copy-start | bytes 786436
  3.7 0.9 %copy-start.7 = (bf16[128,512]{1,0:T(8,128)(2,1)S(1)}, bf16[128,512]{1,0:T(8,128)(2,1)}, u32[]{:S(2)}) copy-start(bf16[128,512]{1,0:T(8,128)(2,1)} %constant.16.clone.fwd_ref) | copy-start | bytes 393220
  5.9 1.4 %collective-permute-start = (f32[2,32,128]{2,1,0:T(8,128)S(1)}, f32[2,32,128]{2,1,0:T(8,128)S(1)}, u32[]{:S(2)}, u32[]{:S(2)}) collective-permute-start(f32[2,32,128]{2,1,0:T(8,128)S(1)} %get-tuple-element.12), channel_id=1, source_target_pairs={{0,1},{1,0},{2,3},{3,2},{4,5},{5,4},{6,7},{7,6},{8,9},{9,8},{10,11... | collective-permute-start | bytes 98312 | tf_op jit(solution)/shard_map/ppermute | solution.py:291
  8.1 8.3 %copy-start.11 = (s32[2,12]{1,0:T(2,128)S(1)}, s32[2,12]{1,0:T(2,128)}, u32[]{:S(2)}) copy-start(s32[2,12]{1,0:T(2,128)} %param.16) | copy-start | bytes 292
  8.1 8.4 %copy-start.10 = (s32[2,12,2]{1,2,0:T(2,128)S(1)}, s32[2,12,2]{1,2,0:T(2,128)}, u32[]{:S(2)}) copy-start(s32[2,12,2]{1,2,0:T(2,128)} %param.17) | copy-start | bytes 580
  8.1 18.5 %all-to-all-start = ((bf16[16,2,32,128]{3,2,1,0:T(8,128)(2,1)}), bf16[16,2,32,128]{3,2,1,0:T(8,128)(2,1)S(1)}, u32[]{:S(2)}, u32[]{:S(2)}) async-start(bf16[16,2,32,128]{3,2,1,0:T(8,128)(2,1)} %reshape.23), calls=%async_computation | async-start | bytes 524288 | tf_op jit(solution)/shard_map/all_to_all | solution.py:295
  26.6 1.4 %copy-start.3 = (bf16[2,128,512]{2,1,0:T(8,128)(2,1)S(1)}, bf16[2,128,512]{2,1,0:T(8,128)(2,1)}, u32[]{:S(2)}) copy-start(bf16[2,128,512]{2,1,0:T(8,128)(2,1)} %targets_ref.1) | copy-start | bytes 786436
  26.6 1.4 %copy-start.4 = (f32[6,64,128]{2,1,0:T(8,128)S(1)}, f32[6,64,128]{2,1,0:T(8,128)}, u32[]{:S(2)}) copy-start(f32[6,64,128]{2,1,0:T(8,128)} %pupils_ref.1) | copy-start | bytes 589828
  26.6 1.4 %copy-start.5 = (bf16[1024,128]{1,0:T(8,128)(2,1)S(1)}, bf16[1024,128]{1,0:T(8,128)(2,1)}, u32[]{:S(2)}) copy-start(bf16[1024,128]{1,0:T(8,128)(2,1)} %constant.19.clone.adj_ref) | copy-start | bytes 786436
  26.6 1.5 %copy-start.6 = (bf16[128,1024]{1,0:T(8,128)(2,1)S(1)}, bf16[128,1024]{1,0:T(8,128)(2,1)}, u32[]{:S(2)}) copy-start(bf16[128,1024]{1,0:T(8,128)(2,1)} %constant.18.clone.inv_ref) | copy-start | bytes 786436
  26.6 1.5 %copy-start.8 = (bf16[128,512]{1,0:T(8,128)(2,1)S(1)}, bf16[128,512]{1,0:T(8,128)(2,1)}, u32[]{:S(2)}) copy-start(bf16[128,512]{1,0:T(8,128)(2,1)} %constant.16.clone.fwd_ref) | copy-start | bytes 393220
  26.7 1.5 %copy-start.9 = (bf16[512,128]{1,0:T(8,128)(2,1)S(1)}, bf16[512,128]{1,0:T(8,128)(2,1)}, u32[]{:S(2)}) copy-start(bf16[512,128]{1,0:T(8,128)(2,1)} %constant.17.clone.points_ref) | copy-start | bytes 393220
  26.8 1.3 %collective-permute-start.1 = (f32[2,32,128]{2,1,0:T(8,128)S(1)}, f32[2,32,128]{2,1,0:T(8,128)S(1)}, u32[]{:S(2)}, u32[]{:S(2)}) collective-permute-start(f32[2,32,128]{2,1,0:T(8,128)S(1)} %shard_map.124.mine_ref), channel_id=1, source_target_pairs={{0,1},{1,0},{2,3},{3,2},{4,5},{5,4},{6,7},{7,6},{8,9},{9,8},{10,11... | collective-permute-start | bytes 98312 | tf_op jit(solution)/shard_map/ppermute | solution.py:291
  34.8 1.3 %collective-permute-start.2 = (f32[2,32,128]{2,1,0:T(8,128)S(1)}, f32[2,32,128]{2,1,0:T(8,128)S(1)}, u32[]{:S(2)}, u32[]{:S(2)}) collective-permute-start(f32[2,32,128]{2,1,0:T(8,128)S(1)} %get-tuple-element.17), channel_id=1, source_target_pairs={{0,1},{1,0},{2,3},{3,2},{4,5},{5,4},{6,7},{7,6},{8,9},{9,8},{10,11... | collective-permute-start | bytes 98312 | tf_op jit(solution)/shard_map/ppermute | solution.py:291
  49.8 1.3 %collective-permute-start.3 = (f32[2,32,128]{2,1,0:T(8,128)S(1)}, f32[2,32,128]{2,1,0:T(8,128)S(1)}, u32[]{:S(2)}, u32[]{:S(2)}) collective-permute-start(f32[2,32,128]{2,1,0:T(8,128)S(1)} %shard_map.127.mine_ref), channel_id=1, source_target_pairs={{0,1},{1,0},{2,3},{3,2},{4,5},{5,4},{6,7},{7,6},{8,9},{9,8},{10,11... | collective-permute-start | bytes 98312 | tf_op jit(solution)/shard_map/ppermute | solution.py:291

commit v2 on v1

--- a/solution.py
+++ b/solution.py
@@ -10,6 +10,7 @@
 from jax.sharding import Mesh
 from jax.sharding import PartitionSpec as P
 
+
 STEEPNESS = 4.0
 THRESHOLD = 1.0
 BF16 = jnp.bfloat16
@@ -19,10 +20,6 @@
 
 def params(limit=VMEM_BYTES):
     return pltpu.CompilerParams(vmem_limit_bytes=limit)
-
-
-def vmem_specs(count):
-    return [pl.BlockSpec(memory_space=pltpu.VMEM)] * count
 
 
 def dft_tables(extent, modes):
@@ -65,21 +62,36 @@
     return jnp.where(left_half(x.shape), -turned, turned)
 
 
-def tile_index(axes):
-    return lax.axis_index(axes[0]) * lax.axis_size(axes[1]) + lax.axis_index(axes[1])
-
-
-def spectrum_kernel(where_ref, masks_ref, br_ref, bc_ref, fwd_ref, keep_ref, send_ref, a_ref, c_ref, full_ref):
+def tile_index():
+    return lax.axis_index("hi") * lax.axis_size("lo") + lax.axis_index("lo")
+
+
+def spectrum_kernel(
+    masks_hbm, br_hbm, bc_hbm, fwd_hbm,
+    keep_ref, send_ref, a_ref, c_ref,
+    full_ref, masks_ref, br_ref, bc_ref, fwd_ref, sems,
+):
     owned, rows, extent = masks_ref.shape
     modes = fwd_ref.shape[0] // 2
     band = modes // 2
-    tile_pos = where_ref[0]
-    side = where_ref[1]
-    own_cols = br_ref[:, pl.ds(pl.multiple_of(tile_pos * rows, rows), rows)]
+    side = lax.axis_index("lo")
+    own = pl.ds(pl.multiple_of(tile_index() * rows, rows), rows)
+    loads = [
+        pltpu.make_async_copy(fwd_hbm, fwd_ref, sems.at[0]),
+        pltpu.make_async_copy(bc_hbm, bc_ref, sems.at[1]),
+        pltpu.make_async_copy(masks_hbm, masks_ref, sems.at[2]),
+        pltpu.make_async_copy(br_hbm.at[:, own], br_ref, sems.at[3]),
+    ]
+    for load in loads:
+        load.start()
+    loads[0].wait()
+    loads[1].wait()
     c = dot(fwd_ref[...], bc_ref[...]).astype(BF16)
-    a = dot(fwd_ref[...], own_cols).astype(BF16)
     c_ref[...] = c
+    loads[3].wait()
+    a = dot(fwd_ref[...], br_ref[...]).astype(BF16)
     a_ref[...] = a
+    loads[2].wait()
     folded = dot_nt(masks_ref[...].reshape(owned * rows, extent), c)
     turned = times_i(folded).astype(BF16)
     folded = folded.astype(BF16)
@@ -90,10 +102,21 @@
     send_ref[...] = full_ref[:, pl.ds(pl.multiple_of((1 - side) * band, band), band), :]
 
 
-def phase_kernel(where_ref, masters_ref, offsets_ref, w1_ref, w2_ref, *, sources, extent):
+def spread_kernel(mine_ref, other_ref, out_ref):
+    owners, halves = out_ref.shape[:2]
+    value = (mine_ref[...] + other_ref[...]).astype(BF16)
+    for d in range(owners):
+        for h in range(halves):
+            out_ref[d, h] = value
+
+
+def phase_kernel(masters_ref, offsets_ref, w1_ref, w2_ref, named_ref, *, extent):
     contexts, masters, band, width = w1_ref.shape
+    sources = masters_ref.shape[1]
+    owned = masters // named_ref.shape[0]
     modes = width // 2
-    side = where_ref[1]
+    side = lax.axis_index("lo")
+    named_ref[...] = jnp.zeros_like(named_ref)
     w1_ref[...] = jnp.zeros_like(w1_ref)
     w2_ref[...] = jnp.zeros_like(w2_ref)
     count = contexts * sources
@@ -104,8 +127,8 @@
     shift_r = jnp.zeros((1, 128), jnp.int32)
     shift_s = jnp.zeros((count, 1), jnp.int32)
     for j in range(count):
-        shift_r = jnp.where(lane == j, offsets_ref[2 * j], shift_r)
-        shift_s = jnp.where(row == j, offsets_ref[2 * j + 1], shift_s)
+        shift_r = jnp.where(lane == j, offsets_ref[j // sources, 0, j % sources], shift_r)
+        shift_s = jnp.where(row == j, offsets_ref[j // sources, 1, j % sources], shift_s)
     angle_u = ((freq_u * shift_r) & (extent - 1)).astype(F32) * step
     lanes = lax.broadcasted_iota(jnp.int32, (count, width), 1)
     freq_v = (lanes & (modes - 1)) - modes // 2
@@ -118,7 +141,8 @@
     for c in range(contexts):
         for j in range(sources):
             i = c * sources + j
-            m = masters_ref[i]
+            m = masters_ref[c, j]
+            named_ref[m // owned, pl.ds(m % owned, 1), :] = jnp.ones((1, width), F32)
             re = jnp.broadcast_to(p_re[:, i : i + 1], (band, width))
             im = jnp.broadcast_to(p_im[:, i : i + 1], (band, width))
             one = slice(i, i + 1)
@@ -162,15 +186,15 @@
 
 
 def image_kernel(
-    where_ref, mine_ref, other_ref, pupils_ref, targets_ref, fwd_ref, points_ref, inv_ref, adj_ref,
+    mine_ref, other_ref, pupils_ref, targets_ref, fwd_ref, points_ref, inv_ref, adj_ref,
     resist_ref, keep_ref, send_ref,
     spec_ref, left_ref, field_ref, pull_ref,
 ):
     kernels, modes, width = pupils_ref.shape
     contexts, rows, extent = targets_ref.shape
     band = modes // 2
-    tile_pos = where_ref[0]
-    side = where_ref[1]
+    tile_pos = tile_index()
+    side = lax.axis_index("lo")
     join_bands(spec_ref, side, mine_ref[...], other_ref[...])
     own = pl.ds(pl.multiple_of(tile_pos * rows, rows), rows)
     points = points_ref[own, :]
@@ -228,41 +252,45 @@
     send_ref[...] = spec_ref[:, pl.ds(pl.multiple_of((1 - side) * band, band), band), :]
 
 
-def scatter_kernel(mine_ref, other_ref, w1_ref, w2_ref, out_ref):
-    owners, halves, owned, band, width = out_ref.shape
-    contexts = w1_ref.shape[0]
+def scatter_kernel(mine_ref, other_ref, w1_ref, w2_ref, named_ref, out_ref):
+    owners, halves, _, width = out_ref.shape
+    contexts, masters, band, _ = w1_ref.shape
+    owned = masters // owners
     grads = [mine_ref[c] + other_ref[c] for c in range(contexts)]
     turned = [swap(grad) for grad in grads]
 
     def body(d, carry):
+        value = jnp.zeros((band, width), F32)
         for m in range(owned):
-            value = jnp.zeros((band, width), F32)
             for c in range(contexts):
                 value = value + grads[c] * w1_ref[c, d * owned + m] + turned[c] * w2_ref[c, d * owned + m]
-            value = value.astype(BF16)
-            for h in range(halves):
-                out_ref[d, h, m] = value
+        value = value.astype(BF16)
+        named = named_ref[d].astype(BF16)
+        for h in range(halves):
+            out_ref[d, h, :band] = value
+            out_ref[d, h, band:] = named
         return carry
 
     over_masters(owners, body, 0)
 
 
 def gather_kernel(got_ref, out_ref):
-    owners, halves, owned, band, width = got_ref.shape
+    owners, halves, _, width = got_ref.shape
+    owned, band, _ = out_ref.shape
 
     def body(d, sums):
-        return tuple(
-            sum((got_ref[d, h, m].astype(F32) for h in range(halves)), sums[m]) for m in range(owned)
-        )
+        value = sum(got_ref[d, h, :band].astype(F32) for h in range(halves))
+        named = got_ref[d, 0, band:].astype(F32)
+        return tuple(sums[m] + value * named[m : m + 1] for m in range(owned))
 
     sums = over_masters(owners, body, (jnp.zeros((band, width), F32),) * owned)
     for m in range(owned):
-        out_ref[m] = sums[m].astype(out_ref.dtype)
-
-
-def lift_kernel(where_ref, mine_ref, other_ref, a_ref, c_ref, out_ref, full_ref):
+        out_ref[m] = sums[m]
+
+
+def lift_kernel(mine_ref, other_ref, a_ref, c_ref, out_ref, full_ref):
     owned = out_ref.shape[0]
-    side = where_ref[1]
+    side = lax.axis_index("lo")
     join_bands(full_ref, side, mine_ref[...], other_ref[...])
     for m in range(owned):
         grad = full_ref[m]
@@ -274,16 +302,16 @@
 def local(masks, blur_rows, blur_cols, pupils, targets, context_masters, offsets):
     owned, rows, extent = masks.shape
     kernels, modes, width = pupils.shape
-    contexts, sources = context_masters.shape
+    contexts, _ = context_masters.shape
     owners = lax.axis_size("ctx")
     halves = lax.axis_size("hi")
     band = modes // 2
     masters = owners * owned
-    tables = dft_tables(extent, modes)
-    forward, points, inverse, adjoint = (jnp.asarray(table) for table in tables)
-    where = jnp.stack([tile_index(("hi", "lo")), lax.axis_index("lo")]).astype(jnp.int32)
+    forward, points, inverse, adjoint = (jnp.asarray(t) for t in dft_tables(extent, modes))
+    flag_rows = 8 * pl.cdiv(owned, 8)
     smem = pl.BlockSpec(memory_space=pltpu.SMEM)
     vmem = pl.BlockSpec(memory_space=pltpu.VMEM)
+    hbm = pl.BlockSpec(memory_space=pltpu.HBM)
     band_f32 = jax.ShapeDtypeStruct((owned, band, width), F32)
     ctx_f32 = jax.ShapeDtypeStruct((contexts, band, width), F32)
 
@@ -295,84 +323,97 @@
         got = lax.all_to_all(flat, ("ctx", "hi"), split_axis=0, concat_axis=0, tiled=True)
         return got.reshape(x.shape)
 
-    keep, send, a_table, c_table = pl.pallas_call(
+    def call(kernel, out_shape, in_specs, *args, scratch=(), flops=1_000_000, limit=VMEM_BYTES):
+        return pl.pallas_call(
+            kernel,
+            out_shape=out_shape,
+            in_specs=in_specs,
+            out_specs=jax.tree.map(lambda _: vmem, out_shape),
+            scratch_shapes=scratch,
+            compiler_params=params(limit),
+            cost_estimate=pl.CostEstimate(flops=flops, bytes_accessed=1_000_000, transcendentals=0),
+        )(*args)
+
+    keep, send, a_table, c_table = call(
         spectrum_kernel,
-        out_shape=(
+        (
             band_f32,
             band_f32,
             jax.ShapeDtypeStruct((width, rows), BF16),
             jax.ShapeDtypeStruct((width, extent), BF16),
         ),
-        in_specs=[smem] + [vmem] * 4,
-        out_specs=(vmem,) * 4,
-        scratch_shapes=[pltpu.VMEM((owned, modes, width), F32)],
-        compiler_params=params(),
-        cost_estimate=pl.CostEstimate(flops=400_000_000, bytes_accessed=2_000_000, transcendentals=0),
-    )(where, masks, blur_rows, blur_cols, forward)
-    spectra = (keep + swap_sides(send)).astype(BF16)
-    outgoing = jnp.broadcast_to(spectra[None, None], (owners, halves, owned, band, width))
-    incoming = exchange(outgoing)
-
+        [hbm] * 4,
+        *(pltpu.with_memory_space_constraint(x, pltpu.HBM) for x in (masks, blur_rows, blur_cols, forward)),
+        scratch=[
+            pltpu.VMEM((owned, modes, width), F32),
+            pltpu.VMEM((owned, rows, extent), BF16),
+            pltpu.VMEM((extent, rows), BF16),
+            pltpu.VMEM((extent, extent), BF16),
+            pltpu.VMEM((width, extent), BF16),
+            pltpu.SemaphoreType.DMA((4,)),
+        ],
+        flops=400_000_000,
+    )
+    other = swap_sides(send)
     w_shape = jax.ShapeDtypeStruct((contexts, masters, band, width), F32)
-    w1, w2 = pl.pallas_call(
-        functools.partial(phase_kernel, sources=sources, extent=extent),
-        out_shape=(w_shape, w_shape),
-        in_specs=[smem] * 3,
-        out_specs=(vmem,) * 2,
-        compiler_params=params(),
-        cost_estimate=pl.CostEstimate(flops=100_000_000, bytes_accessed=1_000_000, transcendentals=0),
-    )(where, context_masters.reshape(-1), offsets.reshape(-1))
-
-    spec = pl.pallas_call(
-        context_kernel,
-        out_shape=ctx_f32,
-        in_specs=[vmem] * 3,
-        out_specs=vmem,
-        compiler_params=params(),
-        cost_estimate=pl.CostEstimate(flops=10_000_000, bytes_accessed=1_000_000, transcendentals=0),
-    )(incoming, w1, w2)
-
-    resist, keep, send = pl.pallas_call(
+    w1, w2, named = call(
+        functools.partial(phase_kernel, extent=extent),
+        (w_shape, w_shape, jax.ShapeDtypeStruct((owners, flag_rows, width), F32)),
+        [smem] * 2,
+        context_masters,
+        jnp.swapaxes(offsets, 1, 2),
+        flops=100_000_000,
+    )
+    outgoing = call(
+        spread_kernel,
+        jax.ShapeDtypeStruct((owners, halves, owned, band, width), BF16),
+        [vmem] * 2,
+        keep,
+        other,
+    )
+    spec = call(context_kernel, ctx_f32, [vmem] * 3, exchange(outgoing), w1, w2)
+    resist, keep, send = call(
         image_kernel,
-        out_shape=(jax.ShapeDtypeStruct((contexts, rows, extent), BF16), ctx_f32, ctx_f32),
-        in_specs=[smem] + [vmem] * 8,
-        out_specs=(vmem,) * 3,
-        scratch_shapes=[
+        (jax.ShapeDtypeStruct((contexts, rows, extent), BF16), ctx_f32, ctx_f32),
+        [vmem] * 8,
+        spec,
+        swap_sides(spec),
+        pupils,
+        targets,
+        forward,
+        points,
+        inverse,
+        adjoint,
+        scratch=[
             pltpu.VMEM((contexts, modes, width), F32),
             pltpu.VMEM((kernels * rows, width), BF16),
             pltpu.VMEM((kernels * rows, 2 * extent), F32),
             pltpu.VMEM((kernels * rows, 2 * extent), BF16),
         ],
-        compiler_params=params(),
-        cost_estimate=pl.CostEstimate(flops=2_000_000_000, bytes_accessed=2_000_000, transcendentals=0),
-    )(where, spec, swap_sides(spec), pupils, targets, forward, points, inverse, adjoint)
-
-    returned = pl.pallas_call(
+        flops=2_000_000_000,
+    )
+    returned = call(
         scatter_kernel,
-        out_shape=jax.ShapeDtypeStruct((owners, halves, owned, band, width), BF16),
-        in_specs=[vmem] * 4,
-        out_specs=vmem,
-        compiler_params=params(),
-        cost_estimate=pl.CostEstimate(flops=10_000_000, bytes_accessed=1_000_000, transcendentals=0),
-    )(keep, swap_sides(send), w1, w2)
-    arrived = exchange(returned)
-    master_grad = pl.pallas_call(
-        gather_kernel,
-        out_shape=band_f32,
-        in_specs=[vmem],
-        out_specs=vmem,
-        compiler_params=params(),
-        cost_estimate=pl.CostEstimate(flops=10_000_000, bytes_accessed=1_000_000, transcendentals=0),
-    )(arrived)
-    mask_grad = pl.pallas_call(
+        jax.ShapeDtypeStruct((owners, halves, band + flag_rows, width), BF16),
+        [vmem] * 5,
+        keep,
+        swap_sides(send),
+        w1,
+        w2,
+        named,
+    )
+    master_grad = call(gather_kernel, band_f32, [vmem], exchange(returned))
+    mask_grad = call(
         lift_kernel,
-        out_shape=jax.ShapeDtypeStruct((owned, rows, extent), F32),
-        in_specs=[smem] + [vmem] * 4,
-        out_specs=vmem,
-        scratch_shapes=[pltpu.VMEM((owned, modes, width), F32)],
-        compiler_params=params(),
-        cost_estimate=pl.CostEstimate(flops=100_000_000, bytes_accessed=1_000_000, transcendentals=0),
-    )(where, master_grad, swap_sides(master_grad), a_table, c_table)
+        jax.ShapeDtypeStruct((owned, rows, extent), F32),
+        [vmem] * 4,
+        master_grad,
+        swap_sides(master_grad),
+        a_table,
+        c_table,
+        scratch=[pltpu.VMEM((owned, modes, width), F32)],
+        flops=100_000_000,
+    )
     return resist, mask_grad
 
 

time: 53.4 us -> 46.9 us (0.88)
  local copies, waits for them, and re-layouts: 5 us -> 0.7 us
  blocking collectives: 13.5 us -> 11.5 us
    unnamed x25 -> x16, local copies, waits for them, and re-layouts: 4.07 us -> 0.7 us
    all_to_all x1, blocking collectives: 13.5 us -> 11.5 us  [exchange(): lax.all_to_all(flat, ('ctx', 'hi'), split_axis=0, concat_axis=0, tiled=True)]
    reshape x3 -> x0, local copies, waits for them, and re-layouts: 0.93 us -> none  [the longest x1 0.75 us: exchange(): flat = x.reshape((owners * halves,) + x.shape[2:])]
    pallas_call x7 -> x8, Pallas kernels: 11.1 us -> 11.6 us  [call(): pl.pallas_call(kernel, out_shape=out_shape, in_specs=in_specs, out_specs=...]
  transfers between devices with their start and end apart: 5 -> 5, of which waited for: 5 -> 5; matrix products, arithmetic and copies ran while one was open for 1% -> 0% of each run, Pallas kernels for 2% -> 2%
where the time goes in v2:
time: 46.9 us; the launch traced here: 46.6 us
  waiting for transfers between devices  12.8 us (27%)
  Pallas kernels  11.6 us (25%)
  blocking collectives  11.5 us (25%)
  starting transfers between devices  9.24 us (20%)
  between operations  0.75 us (2%)
  local copies, waits for them, and re-layouts  0.7 us (1%)
    pallas_call x8, Pallas kernels, call(): pl.pallas_call(kernel, out_shape=out_shape, in_specs=in_specs, out_specs=...  11.6 us
    all_to_all x1, blocking collectives, exchange(): lax.all_to_all(flat, ('ctx', 'hi'), split_axis=0, concat_axis=0, tiled=True)  11.5 us
    all_to_all x1, waiting for transfers between devices, exchange(): lax.all_to_all(flat, ('ctx', 'hi'), split_axis=0, concat_axis=0, tiled=True)  8.48 us
    all_to_all x1, starting transfers between devices, exchange(): lax.all_to_all(flat, ('ctx', 'hi'), split_axis=0, concat_axis=0, tiled=True)  8.32 us
    ppermute x4, waiting for transfers between devices, swap_sides(): return lax.ppermute(x, 'lo', [(0, 1), (1, 0)])  4.3 us
  transfers between devices with their start and end apart: 5, of which 5 were waited for; matrix products, arithmetic and copies ran while one was open for 0% of the time, Pallas kernels for 2%

profile of v2, /device:TPU:0, one launch (start us, length us, event | category | flops | bytes accessed | tf_op | source)
XLA Modules:
  0.0 46.6 jit_solution(12641335900347749223)
XLA Ops:
  0.6 2.1 %shard_map.122 = (f32[2,32,128]{2,1,0:T(8,128)S(1)}, f32[2,32,128]{2,1,0:T(8,128)S(1)}, bf16[128,128]{1,0:T(8,128)(2,1)S(1)}, bf16[128,512]{1,0:T(8,128)(2,1)S(1)}) custom-call(bf16[2,128,512]{2,1,0:T(8,128)(2,1)} %masks_hbm.1, bf16[512,512]{1,0:T(8,128)(2,1)} %br_hbm.1, bf16[512,512]{1,0:T(8,128)(2,1)} %bc_hbm.1, bf16[128,512]{1,0:T(8,128)(2,1)} %constant.8.clone.fwd_hbm.fwd_ref), custom_call_target="tpu_custom_call" | custom-call | flops 400000000 | bytes 1000000 | tf_op jit(solution)/shard_map/pallas_call | solution.py:327
  2.7 0.6 %collective-permute-start = (f32[2,32,128]{2,1,0:T(8,128)S(1)}, f32[2,32,128]{2,1,0:T(8,128)S(1)}, u32[]{:S(2)}, u32[]{:S(2)}) collective-permute-start(f32[2,32,128]{2,1,0:T(8,128)S(1)} %get-tuple-element.13), channel_id=1, source_target_pairs={{0,1},{1,0},{2,3},{3,2},{4,5},{5,4},{6,7},{7,6},{8,9},{9,8},{10,11... | collective-permute-start | bytes 98312 | tf_op jit(solution)/shard_map/ppermute | solution.py:319
  3.3 0.9 %collective-permute-done.other_ref = f32[2,32,128]{2,1,0:T(8,128)S(1)} collective-permute-done((f32[2,32,128]{2,1,0:T(8,128)S(1)}, f32[2,32,128]{2,1,0:T(8,128)S(1)}, u32[]{:S(2)}, u32[]{:S(2)}) %collective-permute-start) | collective-permute-done | bytes 32800 | tf_op jit(solution)/shard_map/ppermute | solution.py:319
  4.1 0.7 %shard_map.123 = bf16[8,2,2,32,128]{4,3,2,1,0:T(8,128)(2,1)} custom-call(f32[2,32,128]{2,1,0:T(8,128)S(1)} %get-tuple-element.12.mine_ref, f32[2,32,128]{2,1,0:T(8,128)S(1)} %collective-permute-done.other_ref), custom_call_target="tpu_custom_call" | custom-call | flops 1000000 | bytes 1000000 | tf_op jit(solution)/shard_map/pallas_call | solution.py:327
  4.9 0.0 copy-start.2
  4.9 8.3 %all-to-all-start = ((bf16[16,2,32,128]{3,2,1,0:T(8,128)(2,1)}), bf16[16,2,32,128]{3,2,1,0:T(8,128)(2,1)S(1)}, u32[]{:S(2)}, u32[]{:S(2)}) async-start(bf16[16,2,32,128]{3,2,1,0:T(8,128)(2,1)} %bitcast), calls=%async_computation | async-start | bytes 524288 | tf_op jit(solution)/shard_map/all_to_all | solution.py:323
  13.2 0.0 copy-start.3
  13.2 0.0 copy-done.2
  13.2 0.7 %copy-done.3 = s32[2,12]{1,0:T(2,128)S(1)} copy-done((s32[2,12]{1,0:T(2,128)S(1)}, s32[2,12]{1,0:T(2,128)}, u32[]{:S(2)}) %copy-start.3) | copy-done | bytes 120
  13.9 1.0 %shard_map.124 = (f32[2,16,32,128]{3,2,1,0:T(8,128)S(1)}, f32[2,16,32,128]{3,2,1,0:T(8,128)S(1)}, f32[8,8,128]{2,1,0:T(8,128)S(1)}) custom-call(s32[2,12]{1,0:T(2,128)S(1)} %copy-done.3, s32[2,2,12]{2,1,0:T(2,128)S(1)} %bitcast.8), custom_call_target="tpu_custom_call" | custom-call | flops 100000000 | bytes 1000000 | tf_op jit(solution)/shard_map/pallas_call | solution.py:327
  14.9 8.5 %all-to-all-done = bf16[16,2,32,128]{3,2,1,0:T(8,128)(2,1)S(1)} async-done(((bf16[16,2,32,128]{3,2,1,0:T(8,128)(2,1)}), bf16[16,2,32,128]{3,2,1,0:T(8,128)(2,1)S(1)}, u32[]{:S(2)}, u32[]{:S(2)}) %all-to-all-start) | async-done | bytes 262176 | tf_op jit(solution)/shard_map/all_to_all | solution.py:323
  23.4 0.0 copy-start
  23.4 0.0 copy-start.1
  23.4 0.0 copy-start.6
  23.4 0.0 copy-start.7
  23.4 0.1 shard_map.125.mine_ref
  23.6 0.1 collective-permute-start.1
  23.7 1.2 %collective-permute-done.1.other_ref = f32[2,32,128]{2,1,0:T(8,128)S(1)} collective-permute-done((f32[2,32,128]{2,1,0:T(8,128)S(1)}, f32[2,32,128]{2,1,0:T(8,128)S(1)}, u32[]{:S(2)}, u32[]{:S(2)}) %collective-permute-start.1) | collective-permute-done | bytes 32800 | tf_op jit(solution)/shard_map/ppermute | solution.py:319
  24.8 0.0 copy-done
  24.8 0.0 copy-done.1
  24.9 0.0 copy-done.4
  24.9 0.0 copy-done.5
  24.9 0.0 copy-done.6
  24.9 0.0 copy-done.7
  24.9 6.2 %shard_map.126 = (bf16[2,128,512]{2,1,0:T(8,128)(2,1)}, f32[2,32,128]{2,1,0:T(8,128)S(1)}, f32[2,32,128]{2,1,0:T(8,128)S(1)}) custom-call(f32[2,32,128]{2,1,0:T(8,128)S(1)} %shard_map.125.mine_ref, f32[2,32,128]{2,1,0:T(8,128)S(1)} %collective-permute-done.1.other_ref, f32[6,64,128]{2,1,0:T(8,128)S(1)} %copy-done.1, bf16[2,128,512]{2,1,0:T(8,128)(2,1)S(1)} %copy-done, ...), custom_call_target="tpu_custom_call" | custom-call | flops 2000000000 | bytes 1000000 | tf_op jit(solution)/shard_map/pallas_call | solution.py:327
  31.1 0.2 collective-permute-start.2
  31.3 1.1 %collective-permute-done.2.other_ref = f32[2,32,128]{2,1,0:T(8,128)S(1)} collective-permute-done((f32[2,32,128]{2,1,0:T(8,128)S(1)}, f32[2,32,128]{2,1,0:T(8,128)S(1)}, u32[]{:S(2)}, u32[]{:S(2)}) %collective-permute-start.2) | collective-permute-done | bytes 32800 | tf_op jit(solution)/shard_map/ppermute | solution.py:319
  32.3 0.1 shard_map.127
  32.5 11.5 %all_to_all.10 = bf16[16,40,128]{2,1,0:T(8,128)(2,1)S(1)} all-to-all(bf16[16,40,128]{2,1,0:T(8,128)(2,1)S(1)} %bitcast.6), channel_id=1, replica_groups=mesh['ctx'=8,'hi'=2,'lo'=2] {'ctx','hi'}, dimensions={0} | all-to-all | bytes 327680 | tf_op jit(solution)/shard_map/all_to_all | solution.py:323
  44.0 0.1 collective-permute-start.3
  44.1 1.2 %collective-permute-done.3.other_ref = f32[2,32,128]{2,1,0:T(8,128)S(1)} collective-permute-done((f32[2,32,128]{2,1,0:T(8,128)S(1)}, f32[2,32,128]{2,1,0:T(8,128)S(1)}, u32[]{:S(2)}, u32[]{:S(2)}) %collective-permute-start.3) | collective-permute-done | bytes 32800 | tf_op jit(solution)/shard_map/ppermute | solution.py:319
  45.3 1.3 %shard_map.129 = f32[2,128,512]{2,1,0:T(8,128)} custom-call(f32[2,32,128]{2,1,0:T(8,128)S(1)} %shard_map.128.mine_ref, f32[2,32,128]{2,1,0:T(8,128)S(1)} %collective-permute-done.3.other_ref, bf16[128,128]{1,0:T(8,128)(2,1)S(1)} %get-tuple-element.20.a_ref, bf16[128,512]{1,0:T(8,128)(2,1)S(1)} %get-tuple-element.21.c_ref), custom_call_target="tpu_custom_call" | custom-call | flops 100000000 | bytes 1000000 | tf_op jit(solution)/shard_map/pallas_call | solution.py:327
  (3 shorter events, 0.0 us)
Async XLA Ops:
  2.7 1.4 %collective-permute-start = (f32[2,32,128]{2,1,0:T(8,128)S(1)}, f32[2,32,128]{2,1,0:T(8,128)S(1)}, u32[]{:S(2)}, u32[]{:S(2)}) collective-permute-start(f32[2,32,128]{2,1,0:T(8,128)S(1)} %get-tuple-element.13), channel_id=1, source_target_pairs={{0,1},{1,0},{2,3},{3,2},{4,5},{5,4},{6,7},{7,6},{8,9},{9,8},{10,11... | collective-permute-start | bytes 98312 | tf_op jit(solution)/shard_map/ppermute | solution.py:319
  4.9 8.3 %copy-start.2 = (s32[2,12,2]{1,2,0:T(2,128)S(1)}, s32[2,12,2]{1,2,0:T(2,128)}, u32[]{:S(2)}) copy-start(s32[2,12,2]{1,2,0:T(2,128)} %param.17) | copy-start | bytes 580
  4.9 18.5 %all-to-all-start = ((bf16[16,2,32,128]{3,2,1,0:T(8,128)(2,1)}), bf16[16,2,32,128]{3,2,1,0:T(8,128)(2,1)S(1)}, u32[]{:S(2)}, u32[]{:S(2)}) async-start(bf16[16,2,32,128]{3,2,1,0:T(8,128)(2,1)} %bitcast), calls=%async_computation | async-start | bytes 524288 | tf_op jit(solution)/shard_map/all_to_all | solution.py:323
  13.2 0.7 %copy-start.3 = (s32[2,12]{1,0:T(2,128)S(1)}, s32[2,12]{1,0:T(2,128)}, u32[]{:S(2)}) copy-start(s32[2,12]{1,0:T(2,128)} %masters_ref.1) | copy-start | bytes 292
  23.4 1.4 %copy-start = (bf16[2,128,512]{2,1,0:T(8,128)(2,1)S(1)}, bf16[2,128,512]{2,1,0:T(8,128)(2,1)}, u32[]{:S(2)}) copy-start(bf16[2,128,512]{2,1,0:T(8,128)(2,1)} %targets_ref.1) | copy-start | bytes 786436
  23.4 1.4 %copy-start.1 = (f32[6,64,128]{2,1,0:T(8,128)S(1)}, f32[6,64,128]{2,1,0:T(8,128)}, u32[]{:S(2)}) copy-start(f32[6,64,128]{2,1,0:T(8,128)} %pupils_ref.1) | copy-start | bytes 589828
  23.4 1.4 %copy-start.4 = (bf16[1024,128]{1,0:T(8,128)(2,1)S(1)}, bf16[1024,128]{1,0:T(8,128)(2,1)}, u32[]{:S(2)}) copy-start(bf16[1024,128]{1,0:T(8,128)(2,1)} %constant.11.clone.adj_ref) | copy-start | bytes 786436
  23.4 1.5 %copy-start.5 = (bf16[128,1024]{1,0:T(8,128)(2,1)S(1)}, bf16[128,1024]{1,0:T(8,128)(2,1)}, u32[]{:S(2)}) copy-start(bf16[128,1024]{1,0:T(8,128)(2,1)} %constant.10.clone.inv_ref) | copy-start | bytes 786436
  23.4 1.5 %copy-start.6 = (bf16[128,512]{1,0:T(8,128)(2,1)S(1)}, bf16[128,512]{1,0:T(8,128)(2,1)}, u32[]{:S(2)}) copy-start(bf16[128,512]{1,0:T(8,128)(2,1)} %constant.8.clone.fwd_hbm.fwd_ref) | copy-start | bytes 393220
  23.4 1.5 %copy-start.7 = (bf16[512,128]{1,0:T(8,128)(2,1)S(1)}, bf16[512,128]{1,0:T(8,128)(2,1)}, u32[]{:S(2)}) copy-start(bf16[512,128]{1,0:T(8,128)(2,1)} %constant.9.clone.points_ref) | copy-start | bytes 393220
  23.6 1.3 %collective-permute-start.1 = (f32[2,32,128]{2,1,0:T(8,128)S(1)}, f32[2,32,128]{2,1,0:T(8,128)S(1)}, u32[]{:S(2)}, u32[]{:S(2)}) collective-permute-start(f32[2,32,128]{2,1,0:T(8,128)S(1)} %shard_map.125.mine_ref), channel_id=1, source_target_pairs={{0,1},{1,0},{2,3},{3,2},{4,5},{5,4},{6,7},{7,6},{8,9},{9,8},{10,11... | collective-permute-start | bytes 98312 | tf_op jit(solution)/shard_map/ppermute | solution.py:319
  31.1 1.3 %collective-permute-start.2 = (f32[2,32,128]{2,1,0:T(8,128)S(1)}, f32[2,32,128]{2,1,0:T(8,128)S(1)}, u32[]{:S(2)}, u32[]{:S(2)}) collective-permute-start(f32[2,32,128]{2,1,0:T(8,128)S(1)} %get-tuple-element.18), channel_id=1, source_target_pairs={{0,1},{1,0},{2,3},{3,2},{4,5},{5,4},{6,7},{7,6},{8,9},{9,8},{10,11... | collective-permute-start | bytes 98312 | tf_op jit(solution)/shard_map/ppermute | solution.py:319
  44.0 1.3 %collective-permute-start.3 = (f32[2,32,128]{2,1,0:T(8,128)S(1)}, f32[2,32,128]{2,1,0:T(8,128)S(1)}, u32[]{:S(2)}, u32[]{:S(2)}) collective-permute-start(f32[2,32,128]{2,1,0:T(8,128)S(1)} %shard_map.128.mine_ref), channel_id=1, source_target_pairs={{0,1},{1,0},{2,3},{3,2},{4,5},{5,4},{6,7},{7,6},{8,9},{9,8},{10,11... | collective-permute-start | bytes 98312 | tf_op jit(solution)/shard_map/ppermute | solution.py:319
